TPU v7x, 32 devices: a whole 2x2x4 slice. The times are simulated.
32 devices in a mesh: dp: 4 (over y, x), blk: 8 (over z, core).
Axes of the slice: x: 2, y: 2, z: 4, core: 2. Of those that a mesh axis runs over, the one named last changes fastest.
Arguments:
- particles: float32 [1024, 1024], P('blk'), may hold values from -14 to 14
- data_rows: bfloat16 [16384, 1024], P('dp'), may hold values from -0.1875 to 0.1875
- labels: int32 [16384], P('dp'), may hold values from 0 to 1
Outputs:
- descent: float32 [1024, 1024], P('blk')
All inputs are finite; a program needn't handle non-finite values.
Results may differ from a plain program's by a relative error of at most 0.0045.
Values may be sent and summed in bfloat16 or wider, within the bound.
A program may use at most 64 MiB of HBM per device.

v0:
```python
import jax
import jax.numpy as jnp
from jax import lax
from jax.sharding import PartitionSpec as P

prior_var = 4.0


def pair_sums(left_x, left_s, right_x, right_s, inv_band):
    feature_count = left_x.shape[1]
    left_xf = left_x.astype(jnp.float32)
    left_sf = left_s.astype(jnp.float32)
    right_xf = right_x.astype(jnp.float32)
    right_sf = right_s.astype(jnp.float32)
    left_norm = jnp.sum(left_xf * left_xf, axis=1)
    right_norm = jnp.sum(right_xf * right_xf, axis=1)
    left_sx = jnp.sum(left_sf * left_xf, axis=1)
    right_sx = jnp.sum(right_sf * right_xf, axis=1)
    gram_xx = jnp.einsum("id,jd->ij", left_x, right_x, preferred_element_type=jnp.float32)
    gram_ss = jnp.einsum("id,jd->ij", left_s, right_s, preferred_element_type=jnp.float32)
    cross_dot = jnp.einsum(
        "id,jd->ij",
        jnp.concatenate([left_x, left_s], axis=1),
        jnp.concatenate([right_s, right_x], axis=1),
        preferred_element_type=jnp.float32,
    )
    distance = left_norm[:, None] + right_norm[None, :] - 2.0 * gram_xx
    kernel = jnp.exp(-0.5 * inv_band * distance)
    bracket = (
        gram_ss
        + inv_band * (left_sx[:, None] - cross_dot + right_sx[None, :])
        + feature_count * inv_band
        - inv_band * inv_band * distance
    )
    weighted_kernel = kernel * bracket
    kernel_sum = jnp.sum(kernel, axis=1)
    weighted_sum = jnp.sum(weighted_kernel, axis=1)
    both_rows = jnp.dot(
        kernel.astype(jnp.bfloat16),
        jnp.concatenate([right_x, right_s], axis=1),
        preferred_element_type=jnp.float32,
    )
    kernel_x = both_rows[:, :feature_count]
    kernel_s = both_rows[:, feature_count:]
    weighted_x = jnp.dot(
        weighted_kernel.astype(jnp.bfloat16), right_x, preferred_element_type=jnp.float32
    )
    return (kernel_sum, weighted_sum, kernel_x, kernel_s, weighted_x)


def forces(left_x, left_s, sums, inv_band, particle_count):
    kernel_sum, weighted_sum, kernel_x, kernel_s, weighted_x = sums
    left_xf = left_x.astype(jnp.float32)
    left_sf = left_s.astype(jnp.float32)
    spread = kernel_sum[:, None] * left_xf - kernel_x
    score_force = (kernel_s + inv_band * spread) / particle_count
    place_force = (
        -inv_band * (weighted_sum[:, None] * left_xf - weighted_x)
        + inv_band * (kernel_sum[:, None] * left_sf - kernel_s)
        - 2.0 * inv_band * inv_band * spread
    ) / particle_count
    return (score_force, place_force)


def empty_sums(rows_count, feature_count):
    flat_zero = jnp.zeros((rows_count,), jnp.float32)
    wide_zero = jnp.zeros((rows_count, feature_count), jnp.float32)
    return (flat_zero, flat_zero, wide_zero, wide_zero, wide_zero)


def pair_folder(left_x, left_s, inv_band, running, pieces):
    pair_parts = pair_sums(left_x, left_s, pieces[0], pieces[1], inv_band)
    return jax.tree.map(jnp.add, running, pair_parts)


def shards(particles, data_rows, labels):
    block_rows, feature_count = particles.shape
    groups_count = lax.axis_size("dp")
    particle_count = block_rows * lax.axis_size("blk")
    inv_band = 1.0 / feature_count
    x_low = particles.astype(jnp.bfloat16)
    logits = jnp.einsum("pd,md->pm", x_low, data_rows, preferred_element_type=jnp.float32)
    probability = jax.nn.sigmoid(logits)
    residual = (labels.astype(jnp.float32)[None, :] - probability).astype(jnp.bfloat16)
    curvature = probability * (1.0 - probability)
    partial_score = jnp.dot(residual, data_rows, preferred_element_type=jnp.float32)
    scores = lax.psum(partial_score, "dp") - particles / prior_var
    s_low = scores.astype(jnp.bfloat16)
    share_rows = block_rows // groups_count
    offset = lax.axis_index("dp") * share_rows
    left_x = lax.dynamic_slice_in_dim(x_low, offset, share_rows, 0)
    left_s = lax.dynamic_slice_in_dim(s_low, offset, share_rows, 0)
    sums = pair_folder(
        left_x,
        left_s,
        inv_band,
        empty_sums(share_rows, feature_count),
        (
            lax.all_gather(x_low, "blk", axis=0, tiled=True),
            lax.all_gather(s_low, "blk", axis=0, tiled=True),
        ),
    )
    score_force, place_force = forces(left_x, left_s, sums, inv_band, particle_count)
    full_force = lax.all_gather(score_force, "dp", axis=0, tiled=True)
    own_place = lax.dynamic_update_slice_in_dim(
        jnp.zeros((block_rows, feature_count), jnp.float32), place_force, offset, 0
    )
    projected = jnp.einsum(
        "pd,md->pm", full_force.astype(jnp.bfloat16), data_rows, preferred_element_type=jnp.float32
    )
    weighted_rows = (curvature * projected).astype(jnp.bfloat16)
    data_term = jnp.dot(weighted_rows, data_rows, preferred_element_type=jnp.float32)
    summed = lax.psum(data_term - own_place, "dp")
    return summed + full_force / prior_var


def solution(mesh):
    placed = (P("blk", None), P("dp", None), P("dp"))
    return jax.shard_map(
        shards, mesh=mesh, in_specs=placed, out_specs=P("blk", None), check_vma=False
    )
```

profile of v0, /device:TPU:0, one launch (start us, length us, event | category | flops | bytes accessed | tf_op | source)
XLA Modules:
  0.0 181.4 jit_solution(16980919114636974199)
XLA Ops:
  7.4 0.0 all-reduce.3.cloned.1.call-start
  7.4 0.7 convert_element_type.42
  8.1 1.1 convert_element_type.38
  9.2 0.0 copy-start.5
  9.2 0.0 copy-start
  9.2 6.5 %fusion.3 = f32[128,4096]{1,0:T(8,128)S(1)} fusion(bf16[128,1024]{1,0:T(8,128)(2,1)S(1)} %convert_element_type.38, bf16[4096,1024]{1,0:T(8,128)(2,1)} %param.4), kind=kOutput, calls=%fused_computation.7 | convolution fusion | flops 1075314688 | bytes 10747904 | tf_op jit(solution)/shard_map/pd,md->pm/dot_general | solution.py:82
  15.7 0.0 copy-done.5
  15.7 0.0 copy-start.2
  15.7 1.3 copy-done.2
  17.0 0.0 copy-done
  17.0 0.0 copy-start.4
  17.0 2.1 %fusion.32 = f32[128,1024]{1,0:T(8,128)} fusion(bf16[4096,1024]{1,0:T(8,128)(2,1)S(1)} %copy-done, f32[128,4096]{1,0:T(8,128)S(1)} %fusion.3, f32[4096]{0:T(1024)S(1)} %convert_element_type.42), kind=kOutput, calls=%fused_computation.36 | convolution fusion | flops 1074790400 | bytes 11026432 | tf_op jit(solution)/shard_map/dot_general | solution.py:86
  19.1 0.0 all-reduce.3.cloned.1.call-update
  19.2 0.0 all-gather.3.cloned.1.call-start
  19.2 0.5 all-gather.3.cloned.1.call-update
  19.7 0.0 all-gather.5.cloned.1.call-start
  19.8 47.6 %all-reduce.3.cloned.1.call-done = f32[128,1024]{1,0:T(8,128)} async-done(((f32[128,1024]{1,0:T(8,128)}), f32[128,1024]{1,0:T(8,128)}) %all-reduce.3.cloned.1.call-update) | async-done | bytes 524304 | tf_op jit(solution)/shard_map/psum | solution.py:87
  67.4 0.0 copy-done.4
  67.4 1.8 subtract_convert_fusion.2
  69.2 0.0 all-gather.5.cloned.1.call-update
  69.2 0.0 all-reduce.5.cloned.1.call-start
  69.3 1.0 fusion.40
  70.3 0.0 all-gather.3.cloned.1.call-done
  70.3 0.0 copy-start.1
  70.3 28.1 %all-gather.5.cloned.1.call-done = bf16[1024,1024]{1,0:T(8,128)(2,1)} async-done(((bf16[128,1024]{1,0:T(8,128)(2,1)}), bf16[1024,1024]{1,0:T(8,128)(2,1)}) %all-gather.5.cloned.1.call-update) | async-done | bytes 2097168 | tf_op jit(solution)/shard_map/all_gather | solution.py:100
  98.4 3.1 %fusion.5 = (f32[1024]{0:T(1024)S(1)}, f32[1024]{0:T(1024)S(1)}) fusion(bf16[1024,1024]{1,0:T(8,128)(2,1)} %all-gather.3.cloned.1.call-done, bf16[1024,1024]{1,0:T(8,128)(2,1)} %all-gather.5.cloned.1.call-done), kind=kLoop, calls=%fused_computation.9 | loop fusion | flops 6289408 | bytes 4202496 | tf_op jit(solution)/shard_map/reduce_sum | solution.py:18
  101.5 0.0 copy-start.3
  101.5 0.0 copy-done.1
  101.6 0.8 fusion.44
  102.4 0.7 copy-done.3
  103.1 0.8 fusion.6
  103.9 0.1 add_multiply_fusion
  104.0 10.0 %all_gather.11 = f32[128,1024]{1,0:T(8,128)S(1)} all-gather(f32[32,1024]{1,0:T(8,128)S(1)} %add_multiply_fusion), channel_id=1, replica_groups=mesh['dp'=4,'blk'=8] {'dp'}, dimensions={0}, use_global_device_ids=true | all-gather | bytes 655360 | tf_op jit(solution)/shard_map/all_gather | solution.py:104
  114.0 1.3 fusion.29
  115.4 0.8 fusion.53
  116.2 0.1 broadcast_in_dim.2
  116.3 0.5 fusion.18
  116.8 11.2 %convolution_subtract_fusion = f32[128,1024]{1,0:T(8,128)} fusion(f32[128,1024]{1,0:T(8,128)S(1)} %fusion.18, bf16[4096,1024]{1,0:T(8,128)(2,1)} %param.4, f32[128,4096]{1,0:T(8,128)} %copy-done.2, f32[128,1024]{1,0:T(8,128)S(1)} %all_gather.11), kind=kOutput, calls=%fused_computation.20 | convolution fusion | flops 2149842944 | bytes 12058624 | tf_op jit(solution)/shard_map/dot_general | solution.py:112
  128.0 0.0 all-reduce.5.cloned.1.call-update
  128.1 44.0 %all-reduce.5.cloned.1.call-done = f32[128,1024]{1,0:T(8,128)} async-done(((f32[128,1024]{1,0:T(8,128)}), f32[128,1024]{1,0:T(8,128)}) %all-reduce.5.cloned.1.call-update) | async-done | bytes 524304 | tf_op jit(solution)/shard_map/psum | solution.py:113
  172.0 1.9 %multiply_add_fusion = f32[128,1024]{1,0:T(8,128)} fusion(f32[128,1024]{1,0:T(8,128)} %all-reduce.5.cloned.1.call-done, f32[128,1024]{1,0:T(8,128)S(1)} %all_gather.11), kind=kLoop, calls=%fused_computation.38 | loop fusion | flops 262144 | bytes 1572864 | tf_op jit(solution)/shard_map/add | solution.py:114
Async XLA Ops:
  7.4 60.0 %all-reduce.3.cloned.1.call-start = ((), (), s32[]{:S(2)}) async-start(), calls=%async_computation.1 | async-start | bytes 1048576 | tf_op jit(solution)/shard_map/psum | solution.py:87
  9.2 6.5 %copy-start.5 = (bf16[128,1024]{1,0:T(8,128)(2,1)}, bf16[128,1024]{1,0:T(8,128)(2,1)S(1)}, u32[]{:S(2)}) copy-start(bf16[128,1024]{1,0:T(8,128)(2,1)S(1)} %convert_element_type.38) | copy-start | bytes 786436
  9.2 7.9 %copy-start = (bf16[4096,1024]{1,0:T(8,128)(2,1)S(1)}, bf16[4096,1024]{1,0:T(8,128)(2,1)}, u32[]{:S(2)}) copy-start(bf16[4096,1024]{1,0:T(8,128)(2,1)} %param.4) | copy-start | bytes 25165828
  15.7 1.4 copy-start.2
  17.0 50.4 %copy-start.4 = (f32[128,1024]{1,0:T(8,128)S(1)}, f32[128,1024]{1,0:T(8,128)}, u32[]{:S(2)}) copy-start(f32[128,1024]{1,0:T(8,128)} %param.3) | copy-start | bytes 1572868
  19.2 51.2 %all-gather.3.cloned.1.call-start = ((), (), s32[]{:S(2)}) async-start(), calls=%async_computation | async-start | bytes 2359296 | tf_op jit(solution)/shard_map/all_gather | solution.py:99
  19.7 78.7 %all-gather.5.cloned.1.call-start = ((), (), s32[]{:S(2)}) async-start(), calls=%async_computation.2 | async-start | bytes 2359296 | tf_op jit(solution)/shard_map/all_gather | solution.py:100
  69.2 102.8 %all-reduce.5.cloned.1.call-start = ((), (), s32[]{:S(2)}) async-start(), calls=%async_computation.3 | async-start | bytes 1048576 | tf_op jit(solution)/shard_map/psum | solution.py:113
  70.3 31.2 %copy-start.1 = (bf16[1024,1024]{1,0:T(8,128)(2,1)S(1)}, bf16[1024,1024]{1,0:T(8,128)(2,1)}, u32[]{:S(2)}) copy-start(bf16[1024,1024]{1,0:T(8,128)(2,1)} %all-gather.3.cloned.1.call-done) | copy-start | bytes 6291460
  101.5 1.6 copy-start.3
Sparse Core Ops, SparseCore 0:
  19.3 48.0 all-reduce.2
  128.2 43.7 all-reduce.4
Sparse Core Ops, SparseCore 1:
  21.2 31.8 all-gather.2
  69.3 29.0 all-gather.4
where the time goes:
time: 182 us; the launch traced here: 181 us
  waiting for transfers between devices  120 us (66%)
  matrix products  24.2 us (13%)
  between operations  15 us (8%)
  blocking collectives  10 us (5%)
  other arithmetic  9.71 us (5%)
  local copies, waits for them, and re-layouts  2.14 us (1%)
    psum x1, waiting for transfers between devices, shards(): scores = lax.psum(partial_score, 'dp') - particles / prior_var  47.6 us
    psum x1, waiting for transfers between devices, shards(): summed = lax.psum(data_term - own_place, 'dp')  44 us
    all_gather x1, waiting for transfers between devices, shards(): lax.all_gather(s_low, 'blk', axis=0, tiled=True)  28.1 us
    dot_general x1, matrix products, shards(): jnp.dot(weighted_rows, data_rows, preferred_element_type=jnp.float32)  11.2 us
    all_gather x1, blocking collectives, shards(): full_force = lax.all_gather(score_force, 'dp', axis=0, tiled=True)  10 us
    dot_general x1, matrix products, shards(): jnp.einsum('pd,md->pm', x_low, data_rows, preferred_element_type=jnp.floa...  6.47 us
  transfers between devices with their start and end apart: 4, of which 3 were waited for; matrix products, arithmetic and copies ran while one was open for 2% of the time, Pallas kernels for 0%

commit v1 on v0

v1 whole, which is shorter than its diff:
```python
import functools

import jax
import jax.numpy as jnp
from jax import lax
from jax.experimental import pallas as pl
from jax.experimental.pallas import tpu as pltpu
from jax.sharding import PartitionSpec as P

MESH = pl.DeviceIdType.MESH
prior_var = 4.0
f32 = jnp.float32
bf16 = jnp.bfloat16
CORES = 2
CHUNKS = 4
TILES = 8


def dot_nn(a, b):
    return jnp.dot(a, b, preferred_element_type=f32)


def dot_nt(a, b):
    return lax.dot_general(a, b, (((1,), (1,)), ((), ())), preferred_element_type=f32)


def remote(src, dst, send, recv, device):
    return pltpu.make_async_remote_copy(
        src_ref=src, dst_ref=dst, send_sem=send, recv_sem=recv, device_id=device, device_id_type=MESH
    )


def kernel(
    n, nb, part_ref, lab_ref, data_hbm, out_ref,
    data, curv, rows_low, x_low, x_all, s_all, s_own, psf, kx, ks, g_own, g_all, o_all,
    s_out, g_out, o_out, s_in, g_in, o_in,
    load_sem, xz, xf, sr, sa, sz, sf, gr, ga, orr, oa,
):
    rows, width = part_ref.shape
    share = rows // n
    nz = nb // CORES
    cw = width // CHUNKS
    tile = data_hbm.shape[0] // TILES
    total = rows * nb
    pairs = share * nb
    c_band = 1.0 / width
    dp = lax.axis_index("dp")
    blk = lax.axis_index("blk")
    zi, core = blk // CORES, lax.rem(blk, CORES)
    own = pl.ds(pl.multiple_of(dp * share, share), share)
    mine = pl.ds(pl.multiple_of(blk * share, share), share)
    partner = (dp, zi * CORES + 1 - core)

    def dp_dev(p):
        return lax.rem(dp + p, n)

    def z_dev(q):
        return lax.rem(zi + q, nz) * CORES + core

    def share_of(index):
        return pl.ds(pl.multiple_of(index * share, share), share)

    def load(t):
        piece = pl.ds(t * tile, tile)
        return pltpu.make_async_copy(data_hbm.at[piece], data.at[piece], load_sem.at[t])

    for t in range(TILES):
        load(t).start()

    barrier = pltpu.get_barrier_semaphore()
    for p in range(1, n):
        pl.semaphore_signal(barrier, inc=1, device_id=(dp_dev(p), blk), device_id_type=MESH)
    for q in range(1, nz):
        pl.semaphore_signal(barrier, inc=1, device_id=(dp, z_dev(q)), device_id_type=MESH)
    pl.semaphore_signal(barrier, inc=1, device_id=partner, device_id_type=MESH)
    x_low[...] = part_ref[...].astype(bf16)
    x_all[mine, :] = part_ref[own, :].astype(bf16)
    pl.semaphore_wait(barrier, n - 1 + nz - 1 + 1)

    sent = []

    def go(copy):
        copy.start()
        sent.append(copy)

    def arrived(place, sems, index, device):
        remote(place, place, sems[0].at[index], sems[1].at[index], device).wait_recv()

    for q in range(1, nz):
        go(remote(x_all.at[mine], x_all.at[mine], xz[0].at[q - 1], xz[1].at[q - 1], (dp, z_dev(q))))
    go(remote(x_all.at[mine], x_all.at[mine], xf[0].at[0], xf[1].at[0], partner))

    def logit_step(t, carry):
        piece = pl.ds(pl.multiple_of(t * tile, tile), tile)
        load(t).wait()
        probability = jax.nn.sigmoid(dot_nt(x_low[...], data[piece, :]))
        curv[:, piece] = probability * (1.0 - probability)
        rows_low[:, piece] = (lab_ref[:, piece].astype(f32) - probability).astype(bf16)
        return carry

    lax.fori_loop(0, TILES, logit_step, 0)

    for q in range(1, nz):
        slot = share_of(lax.rem(zi + nz - q, nz) * CORES + core)
        arrived(x_all.at[slot], xz, q - 1, partner)
        go(remote(x_all.at[slot], x_all.at[slot], xf[0].at[q], xf[1].at[q], partner))

    def scatter(c, buffer, landing, sems):
        for p in range(1, n):
            to = dp_dev(p)
            go(remote(buffer.at[c, share_of(to)], landing.at[c, p - 1],
                      sems[0].at[c, p - 1], sems[1].at[c, p - 1], (to, blk)))

    def reduced(c, landing, sems):
        value = psf[c, own, :]
        for p in range(1, n):
            arrived(landing.at[c, p - 1], sems, (c, p - 1), partner)
            value = value + landing[c, p - 1].astype(f32)
        return value

    def gather(c, buffer, sems):
        for p in range(1, n):
            go(remote(buffer.at[c, own], buffer.at[c, own],
                      sems[0].at[c, p - 1], sems[1].at[c, p - 1], (dp_dev(p), blk)))

    def gathered(c, buffer, sems):
        for p in range(1, n):
            arrived(buffer.at[c, share_of(dp_dev(n - p))], sems, (c, p - 1), partner)

    for c in range(CHUNKS):
        cols = slice(c * cw, (c + 1) * cw)
        partial = dot_nn(rows_low[...], data[:, cols])
        psf[c] = partial
        s_out[c] = partial.astype(bf16)
        scatter(c, s_out, s_in, sr)

    for q in range(nz):
        slot = share_of(lax.rem(zi + nz - q, nz) * CORES + 1 - core)
        arrived(x_all.at[slot], xf, q, partner)
    right_xf = x_all[...].astype(f32)
    left_xf = x_low[...].astype(f32)
    right_norm = jnp.broadcast_to(jnp.sum(right_xf * right_xf, axis=1, keepdims=True), (pairs, rows)).T
    left_norm = jnp.sum(left_xf * left_xf, axis=1, keepdims=True)
    distance = left_norm + right_norm - 2.0 * dot_nt(x_low[...], x_all[...])
    kern = jnp.exp(-0.5 * c_band * distance)
    kernel_sum = jnp.sum(kern, axis=1, keepdims=True)
    kern_low = kern.astype(bf16)
    for c in range(CHUNKS):
        cols = slice(c * cw, (c + 1) * cw)
        kx[c] = dot_nn(kern_low, x_all[:, cols])

    for c in range(CHUNKS):
        cols = slice(c * cw, (c + 1) * cw)
        score = reduced(c, s_in, sr) - part_ref[own, cols] / prior_var
        score_low = score.astype(bf16)
        s_all[c, mine, :] = score_low
        s_own[c, own, :] = score_low
        for q in range(1, nz):
            go(remote(s_all.at[c, mine], s_all.at[c, mine], sz[0].at[c, q - 1], sz[1].at[c, q - 1], (dp, z_dev(q))))
        go(remote(s_all.at[c, mine], s_all.at[c, mine], sf[0].at[c, 0], sf[1].at[c, 0], partner))
        gather(c, s_own, sa)

    def push_force(c):
        cols = slice(c * cw, (c + 1) * cw)
        for q in range(nz):
            slot = share_of(lax.rem(zi + nz - q, nz) * CORES + 1 - core)
            arrived(s_all.at[c, slot], sf, (c, q), partner)
        kernel_s = dot_nn(kern_low, s_all[c])
        ks[c] = kernel_s
        spread = kernel_sum * x_low[:, cols].astype(f32) - kx[c]
        force = (kernel_s + c_band * spread) / total
        psf[c] = force
        g_out[c] = force.astype(bf16)
        scatter(c, g_out, g_in, gr)

    for c in range(CHUNKS):
        for q in range(1, nz):
            slot = share_of(lax.rem(zi + nz - q, nz) * CORES + core)
            arrived(s_all.at[c, slot], sz, (c, q - 1), partner)
            go(remote(s_all.at[c, slot], s_all.at[c, slot], sf[0].at[c, q], sf[1].at[c, q], partner))
        if c:
            push_force(c - 1)

    push_force(CHUNKS - 1)

    for c in range(CHUNKS):
        force = reduced(c, g_in, gr)
        g_own[c] = force
        g_all[c, own, :] = force.astype(bf16)
        gather(c, g_all, ga)

    bracket = width * c_band - c_band * c_band * distance
    gram_ss = jnp.zeros((rows, pairs), f32)
    cross = jnp.zeros((rows, pairs), f32)
    left_sx = jnp.zeros((rows, 1), f32)
    right_sx = jnp.zeros((pairs, 1), f32)
    for c in range(CHUNKS):
        cols = slice(c * cw, (c + 1) * cw)
        gathered(c, s_own, sa)
        left_s, right_s = s_own[c], s_all[c]
        gram_ss += dot_nt(left_s, right_s)
        cross += dot_nt(x_low[:, cols], right_s) + dot_nt(left_s, x_all[:, cols])
        left_sx += jnp.sum(left_s.astype(f32) * x_low[:, cols].astype(f32), axis=1, keepdims=True)
        right_sx += jnp.sum(right_s.astype(f32) * x_all[:, cols].astype(f32), axis=1, keepdims=True)
    bracket += gram_ss + c_band * (left_sx - cross + jnp.broadcast_to(right_sx, (pairs, rows)).T)
    weighted = kern * bracket
    weighted_sum = jnp.sum(weighted, axis=1, keepdims=True)
    weighted_low = weighted.astype(bf16)
    for c in range(CHUNKS):
        cols = slice(c * cw, (c + 1) * cw)
        left_x = x_low[:, cols].astype(f32)
        wx = dot_nn(weighted_low, x_all[:, cols])
        spread = kernel_sum * left_x - kx[c]
        kx[c] = (
            -c_band * (weighted_sum * left_x - wx)
            + c_band * (kernel_sum * s_own[c].astype(f32) - ks[c])
            - 2.0 * c_band * c_band * spread
        ) / total

    for c in range(CHUNKS):
        gathered(c, g_all, ga)

    def project_step(t, carry):
        piece = pl.ds(pl.multiple_of(t * tile, tile), tile)
        force = jnp.concatenate([g_all[c] for c in range(CHUNKS)], axis=1)
        projected = dot_nt(force, data[piece, :])
        rows_low[:, piece] = (curv[:, piece] * projected).astype(bf16)
        return carry

    lax.fori_loop(0, TILES, project_step, 0)

    for c in range(CHUNKS):
        cols = slice(c * cw, (c + 1) * cw)
        partial = dot_nn(rows_low[...], data[:, cols]) - kx[c]
        psf[c] = partial
        o_out[c] = partial.astype(bf16)
        scatter(c, o_out, o_in, orr)

    for c in range(CHUNKS):
        value = reduced(c, o_in, orr) + g_own[c] / prior_var
        o_all[c, own, :] = value.astype(bf16)
        gather(c, o_all, oa)

    for c in range(CHUNKS):
        gathered(c, o_all, oa)
        out_ref[:, c * cw:(c + 1) * cw] = o_all[c]
    for copy in sent:
        copy.wait_send()


def solution(mesh):
    n, nb = mesh.shape["dp"], mesh.shape["blk"]
    nz = nb // CORES

    def shards(particles, data_rows, labels):
        rows, width = particles.shape
        examples = data_rows.shape[0]
        share, cw, pairs = rows // n, width // CHUNKS, rows // n * nb
        V, D = pltpu.VMEM, pltpu.SemaphoreType.DMA

        def two(*shape):
            return [D(shape), D(shape)]

        result = pl.pallas_call(
            functools.partial(kernel, n, nb),
            out_shape=jax.ShapeDtypeStruct((rows, width), bf16),
            in_specs=[pl.BlockSpec(memory_space=V), pl.BlockSpec(memory_space=V), pl.BlockSpec(memory_space=pl.ANY)],
            out_specs=pl.BlockSpec(memory_space=V),
            scratch_shapes=[
                V((examples, width), bf16),
                V((rows, examples), f32),
                V((rows, examples), bf16),
                V((rows, width), bf16),
                V((pairs, width), bf16),
                V((CHUNKS, pairs, cw), bf16),
                V((CHUNKS, rows, cw), bf16),
                V((CHUNKS, rows, cw), f32),
                V((CHUNKS, rows, cw), f32),
                V((CHUNKS, rows, cw), f32),
                V((CHUNKS, share, cw), f32),
                V((CHUNKS, rows, cw), bf16),
                V((CHUNKS, rows, cw), bf16),
                V((CHUNKS, rows, cw), bf16),
                V((CHUNKS, rows, cw), bf16),
                V((CHUNKS, rows, cw), bf16),
                V((CHUNKS, n - 1, share, cw), bf16),
                V((CHUNKS, n - 1, share, cw), bf16),
                V((CHUNKS, n - 1, share, cw), bf16),
                D((TILES,)),
                two(nz - 1),
                two(nz),
                two(CHUNKS, n - 1),
                two(CHUNKS, n - 1),
                two(CHUNKS, nz - 1),
                two(CHUNKS, nz),
                two(CHUNKS, n - 1),
                two(CHUNKS, n - 1),
                two(CHUNKS, n - 1),
                two(CHUNKS, n - 1),
            ],
            compiler_params=pltpu.CompilerParams(
                collective_id=0, has_side_effects=True, vmem_limit_bytes=56 * 1024 * 1024
            ),
        )(particles, labels.reshape(1, examples), data_rows)
        return result.astype(f32)

    placed = (P("blk", None), P("dp", None), P("dp"))
    return jax.shard_map(shards, mesh=mesh, in_specs=placed, out_specs=P("blk", None), check_vma=False)
```

time: 182 us -> 50.1 us (0.28)
  waiting for transfers between devices: 120 us -> 0 us
  Pallas kernels: 0 us -> 48.1 us
  matrix products: 24.2 us -> 0 us
  between operations: 15 us -> 0.01 us
  blocking collectives: 10 us -> 0 us
  other arithmetic: 9.71 us -> 1.79 us
  local copies, waits for them, and re-layouts: 2.14 us -> 0 us
    psum x2 -> x0, waiting for transfers between devices: 91.6 us -> none  [the longest x1 47.6 us: shards(): scores = lax.psum(partial_score, 'dp') - particles / prior_var]
    pallas_call x0 -> x1, Pallas kernels: none -> 48.1 us  [shards(): pl.pallas_call(functools.partial(kernel, n, nb), out_shape=jax.ShapeDtype...]
    all_gather x2 -> x0, waiting for transfers between devices: 28.1 us -> none  [the longest x1 28.1 us: shards(): lax.all_gather(s_low, 'blk', axis=0, tiled=True)]
    dot_general x8 -> x0, matrix products: 24.2 us -> none  [the longest x1 11.2 us: shards(): jnp.dot(weighted_rows, data_rows, preferred_element_type=jnp.float32)]
    all_gather x1 -> x0, blocking collectives: 10 us -> none  [shards(): full_force = lax.all_gather(score_force, 'dp', axis=0, tiled=True)]
    reduce_sum x2 -> x0, other arithmetic: 4.12 us -> none  [the longest x1 3.11 us: pair_sums(): right_sx = jnp.sum(right_sf * right_xf, axis=1)]
    unnamed x12 -> x0, local copies, waits for them, and re-layouts: 2.09 us -> none
    add x1 -> x0, other arithmetic: 1.89 us -> none  [shards(): return summed + full_force / prior_var]
  transfers between devices with their start and end apart: 4 -> 0, of which waited for: 3 -> 0; matrix products, arithmetic and copies ran while one was open for 2% -> 0% of each run, Pallas kernels for 0% -> 0%
where the time goes in v1:
time: 50.1 us; the launch traced here: 49.9 us
  Pallas kernels  48.1 us (96%)
  other arithmetic  1.79 us (4%)
    pallas_call x1, Pallas kernels, shards(): pl.pallas_call(functools.partial(kernel, n, nb), out_shape=jax.ShapeDtype...  48.1 us
    convert_element_type x1, other arithmetic, shards(): return result.astype(f32)  1.79 us

profile of v1, /device:TPU:0, one launch (start us, length us, event | category | flops | bytes accessed | tf_op | source)
XLA Modules:
  0.0 49.9 jit_solution(13776309057227991889)
XLA Ops:
  0.0 48.1 %shard_map.37 = bf16[128,1024]{1,0:T(8,128)(2,1)} custom-call(f32[128,1024]{1,0:T(8,128)} %part_ref.1, s32[1,4096]{1,0:T(1,128)} %bitcast.1, bf16[4096,1024]{1,0:T(8,128)(2,1)} %data_hbm.1), custom_call_target="tpu_custom_call" | custom-call | tf_op jit(solution)/shard_map/pallas_call | solution.py:264
  48.1 1.8 %convert_element_type.3 = f32[128,1024]{1,0:T(8,128)} convert(bf16[128,1024]{1,0:T(8,128)(2,1)} %shard_map.37) | non-fusion elementwise | flops 131072 | bytes 786432 | tf_op jit(solution)/shard_map/convert_element_type | solution.py:305
